TPU v7x, 32 devices: a 4x4x1 block of a 4x4x8 slice. The times are simulated.
32 devices in a mesh: rep: 1 (over z), data: 4 (over y), expert: 8 (over x, core).
Axes of the slice: x: 4, y: 4, z: 1, core: 2. Of those that a mesh axis runs over, the one named last changes fastest.
The devices are a block of a 4x4x8 slice.
Arguments:
- x_in: bfloat16 [2, 16384, 2048], P(None, ('rep', 'expert', 'data'))
- expert_idx: int32 [2, 16384, 6], P(None, ('rep', 'expert', 'data'))
- gate_wt: float32 [2, 16384, 6], P(None, ('rep', 'expert', 'data'))
- w_gate: bfloat16 [64, 2048, 1408], P('expert', 'data')
- w_up: bfloat16 [64, 2048, 1408], P('expert', 'data')
- w_down: bfloat16 [64, 1408, 2048], P('expert', None, 'data')
Outputs:
- output: bfloat16 [2, 16384, 2048], P(None, ('rep', 'expert', 'data'))
All inputs are finite; a program needn't handle non-finite values.
Results may differ from a plain program's by a relative error of at most 0.00131.
Values are sent between devices in bfloat16 or wider.
A program may use at most 768 MiB of HBM per device.

v0:
```python
import jax
import jax.numpy as jnp
from jax import lax
from jax.sharding import PartitionSpec as P, NamedSharding


def dispatch_block(x_blk, ids_blk, n_exp, capacity):
    tok_loc, n_top = ids_blk.shape
    pair_count = tok_loc * n_top
    slot_total = n_exp * capacity
    flat_ids = ids_blk.reshape(pair_count)
    one_hot = (flat_ids[:, None] == jnp.arange(n_exp, dtype=jnp.int32)[None, :]).astype(jnp.int32)
    slot_of = jnp.sum((jnp.cumsum(one_hot, axis=0) - one_hot) * one_hot, axis=1)
    is_kept = slot_of < capacity
    dest_pos = jnp.where(is_kept, flat_ids * capacity + slot_of, slot_total)
    source_of = jnp.full((slot_total,), pair_count, jnp.int32).at[dest_pos].set(jnp.arange(pair_count, dtype=jnp.int32), mode='drop')
    tok_of = jnp.minimum(source_of // n_top, tok_loc - 1)
    send_rows = jnp.where((source_of < pair_count)[:, None], jnp.take(x_blk, tok_of, axis=0), jnp.zeros((), x_blk.dtype))
    return send_rows, dest_pos, is_kept


def combine_block(x_blk, gate_blk, back_rows, dest_pos, is_kept):
    tok_loc, n_top = gate_blk.shape
    slot_total = back_rows.shape[0]
    pair_out = jnp.take(back_rows, jnp.minimum(dest_pos, slot_total - 1), axis=0).reshape(tok_loc, n_top, -1)
    weight = jnp.where(is_kept.reshape(tok_loc, n_top), gate_blk, 0.0)
    mix_sum = jnp.sum(pair_out.astype(jnp.float32) * weight[:, :, None], axis=1)
    return (x_blk.astype(jnp.float32) + mix_sum).astype(jnp.bfloat16)


def expert_mlp(rows_in, wg_full, wu_full, wd_full):
    gate_pre = jnp.einsum('lrd,ldf->lrf', rows_in, wg_full, preferred_element_type=jnp.float32)
    up_pre = jnp.einsum('lrd,ldf->lrf', rows_in, wu_full, preferred_element_type=jnp.float32)
    hidden = (jax.nn.silu(gate_pre) * up_pre).astype(jnp.bfloat16)
    return jnp.einsum('lrf,lfd->lrd', hidden, wd_full, preferred_element_type=jnp.float32).astype(jnp.bfloat16)


def solution(mesh):
    expert_devs = mesh.shape['expert']
    row_spec = P(None, ('rep', 'expert', 'data'), None)
    up_spec = P('expert', 'data', None)
    down_spec = P('expert', None, 'data')

    def per_device(x_loc, idx_loc, gate_loc, wg_loc, wu_loc, wd_loc):
        n_loc = wg_loc.shape[0]
        n_exp = n_loc * expert_devs
        d_model = x_loc.shape[2]
        tok_loc = idx_loc.shape[1]
        n_top = idx_loc.shape[2]
        capacity = 8 * ((5 * n_top * tok_loc + 32 * n_exp - 1) // (32 * n_exp))
        wg_full = lax.all_gather(wg_loc, 'data', axis=1, tiled=True)
        wu_full = lax.all_gather(wu_loc, 'data', axis=1, tiled=True)
        wd_full = lax.all_gather(wd_loc, 'data', axis=2, tiled=True)
        results = []
        for mb_index in range(x_loc.shape[0]):
            send_rows, dest_pos, is_kept = dispatch_block(x_loc[mb_index], idx_loc[mb_index], n_exp, capacity)
            recv_rows = lax.all_to_all(send_rows.reshape(expert_devs, n_loc, capacity, d_model), 'expert', 0, 2, tiled=True)
            out_rows = expert_mlp(recv_rows.reshape(n_loc, expert_devs * capacity, d_model), wg_full, wu_full, wd_full)
            back_rows = lax.all_to_all(out_rows.reshape(1, n_loc, expert_devs * capacity, d_model), 'expert', 2, 0, tiled=True)
            results.append(combine_block(x_loc[mb_index], gate_loc[mb_index], back_rows.reshape(n_exp * capacity, d_model), dest_pos, is_kept))
        return jnp.stack(results)

    return jax.shard_map(per_device, mesh=mesh, in_specs=(row_spec, row_spec, row_spec, up_spec, up_spec, down_spec), out_specs=row_spec, check_vma=False)
```

profile of v0, /device:TPU:104, one launch (start us, length us, event | category | flops | bytes accessed | tf_op | source)
XLA Modules:
  0.0 1784.0 jit_solution(8570825937441939986)
XLA Ops:
  6.6 0.7 all-gather.4.cloned.1.call-update
  7.4 0.7 all-gather.6.cloned.1.call-update
  8.2 0.7 all-gather.8.cloned.1.call-update
  9.5 18.3 %reduce-window.16 = s32[64,24,128]{2,1,0:T(8,128)S(1)} reduce-window(s32[64,24,128]{2,1,0:T(8,128)S(1)} %fusion.9, s32[]{:T(128)} %constant.33.clone.1), window={size=1x1x128 pad=0_0x0_0x127_0}, to_apply=%region_5.8 | reduce-window | flops 24969216 | bytes 1572868 | tf_op jit(solution)/shard_map/reduce-window.2
  29.6 0.6 copy-done.5
  30.2 11.8 scatter_custom_fusion.1
  42.1 4.0 slice_bitcast_fusion.1
  46.1 33.2 %gather_fusion.2 = bf16[4096,2048]{1,0:T(8,128)(2,1)} fusion(bf16[512,2048]{1,0:T(8,128)(2,1)} %get-tuple-element.10, s32[4096]{0:T(1024)S(1)} %broadcast_clamp_fusion), kind=kCustom, calls=%fused_computation.2.clone | custom fusion | bytes 33570816 | tf_op jit(solution)/shard_map/jit(_take)/gather | solution.py:18
  79.3 15.1 select_select_fusion
  94.4 5.9 all-to-all-start.2
  100.8 0.9 fusion.8
  101.7 31.9 %reduce-window.14 = s32[64,24,128]{2,1,0:T(8,128)S(1)} reduce-window(s32[64,24,128]{2,1,0:T(8,128)} %fusion.8, s32[]{:T(128)} %constant.33.clone.1), window={size=1x1x128 pad=0_0x0_0x127_0}, to_apply=%region_0.0 | reduce-window | flops 24969216 | bytes 1572868 | tf_op jit(solution)/shard_map/reduce-window
  133.6 1.2 slice.50
  134.8 1.6 copy.71
  137.4 11.8 scatter_custom_fusion
  149.3 21.0 %gather_fusion = bf16[4096,2048]{1,0:T(8,128)(2,1)} fusion(bf16[512,2048]{1,0:T(8,128)(2,1)S(1)} %get-tuple-element.9, s32[4096]{0:T(1024)S(1)} %broadcast_clamp_fusion.1), kind=kCustom, calls=%fused_computation.clone | custom fusion | bytes 33570816 | tf_op jit(solution)/shard_map/jit(_take)/gather | solution.py:18
  170.2 15.0 select_select_fusion.1
  185.3 99.3 %all-to-all-done.2 = bf16[8,8,64,2048]{3,2,1,0:T(8,128)(2,1)} async-done(((bf16[8,8,64,2048]{3,2,1,0:T(8,128)(2,1)}), bf16[8,8,64,2048]{3,2,1,0:T(8,128)(2,1)}, u32[]{:S(2)}, u32[]{:S(2)}) %all-to-all-start.2) | async-done | bytes 16777248 | tf_op jit(solution)/shard_map/all_to_all | solution.py:57
  284.5 6.1 all-to-all-start
  290.7 14.2 copy.66
  304.8 170.1 %all-to-all-done = bf16[8,8,64,2048]{3,2,1,0:T(8,128)(2,1)} async-done(((bf16[8,8,64,2048]{3,2,1,0:T(8,128)(2,1)}), bf16[8,8,64,2048]{3,2,1,0:T(8,128)(2,1)}, u32[]{:S(2)}, u32[]{:S(2)}) %all-to-all-start) | async-done | bytes 16777248 | tf_op jit(solution)/shard_map/all_to_all | solution.py:57
  475.0 14.2 copy.56
  489.1 40.6 %fusion.21 = f32[8,512,1408]{2,1,0:T(8,128)} fusion(bf16[8,512,2048]{2,1,0:T(8,128)(2,1)} %bitcast.101, bf16[8,2048,1408]{2,1,0:T(8,128)(2,1)} %all-gather.4.cloned.1.call-done), kind=kOutput, calls=%fused_computation.80 | convolution fusion | flops 23622320128 | bytes 85983232 | tf_op jit(solution)/shard_map/lrd,ldf->lrf/dot_general | solution.py:32
  529.7 275.2 %all-gather.6.cloned.1.call-done = bf16[8,2048,1408]{2,1,0:T(8,128)(2,1)} async-done(((bf16[8,512,1408]{2,1,0:T(8,128)(2,1)}), bf16[8,2048,1408]{2,1,0:T(8,128)(2,1)}) %all-gather.6.cloned.1.call-update) | async-done | bytes 46137360 | tf_op jit(solution)/shard_map/all_gather | solution.py:52
  804.9 38.1 %multiply_convert_fusion = bf16[8,512,1408]{2,1,0:T(8,128)(2,1)} fusion(f32[8,512,1408]{2,1,0:T(8,128)} %fusion.21, bf16[8,512,2048]{2,1,0:T(8,128)(2,1)} %bitcast.102, bf16[8,2048,1408]{2,1,0:T(8,128)(2,1)} %all-gather.6.cloned.1.call-done), kind=kOutput, calls=%fused_computation.8 | convolution fusion | flops 23656923136 | bytes 97517568 | tf_op jit(solution)/shard_map/lrd,ldf->lrf/dot_general | solution.py:33
  843.0 360.5 %all-gather.8.cloned.1.call-done = bf16[8,1408,2048]{2,1,0:T(8,128)(2,1)} async-done(((bf16[8,1408,512]{2,1,0:T(8,128)(2,1)}), bf16[8,1408,2048]{2,1,0:T(8,128)(2,1)}) %all-gather.8.cloned.1.call-update) | async-done | bytes 46137360 | tf_op jit(solution)/shard_map/all_gather | solution.py:53
  1203.5 35.9 %convert_bitcast_fusion = bf16[1,8,512,2048]{3,2,1,0:T(8,128)(2,1)} fusion(bf16[8,512,1408]{2,1,0:T(8,128)(2,1)} %multiply_convert_fusion, bf16[8,1408,2048]{2,1,0:T(8,128)(2,1)} %all-gather.8.cloned.1.call-done), kind=kOutput, calls=%fused_computation.12 | convolution fusion | flops 23630708736 | bytes 74448896 | tf_op jit(solution)/shard_map/lrf,lfd->lrd/dot_general | solution.py:35
  1239.5 18.6 %copy.67 = bf16[1,8,512,2048]{3,1,0,2:T(8,128)(2,1)} copy(bf16[1,8,512,2048]{3,2,1,0:T(8,128)(2,1)} %convert_bitcast_fusion) | data formatting | bytes 33554432 | tf_op jit(solution)/shard_map/reshape | solution.py:59
  1258.1 6.1 all-to-all-start.3
  1264.2 40.7 %fusion.20 = f32[8,512,1408]{2,1,0:T(8,128)} fusion(bf16[8,512,2048]{2,1,0:T(8,128)(2,1)} %bitcast.99, bf16[8,2048,1408]{2,1,0:T(8,128)(2,1)} %all-gather.4.cloned.1.call-done), kind=kOutput, calls=%fused_computation.79 | convolution fusion | flops 23622320128 | bytes 85983232 | tf_op jit(solution)/shard_map/lrd,ldf->lrf/dot_general | solution.py:32
  1304.9 38.1 %multiply_convert_fusion.1 = bf16[8,512,1408]{2,1,0:T(8,128)(2,1)} fusion(f32[8,512,1408]{2,1,0:T(8,128)} %fusion.20, bf16[8,512,2048]{2,1,0:T(8,128)(2,1)} %bitcast.100, bf16[8,2048,1408]{2,1,0:T(8,128)(2,1)} %all-gather.6.cloned.1.call-done), kind=kOutput, calls=%fused_computation.9 | convolution fusion | flops 23656923136 | bytes 97517568 | tf_op jit(solution)/shard_map/lrd,ldf->lrf/dot_general | solution.py:33
  1343.0 35.7 %convert_bitcast_fusion.1 = bf16[1,8,512,2048]{3,2,1,0:T(8,128)(2,1)} fusion(bf16[8,512,1408]{2,1,0:T(8,128)(2,1)} %multiply_convert_fusion.1, bf16[8,1408,2048]{2,1,0:T(8,128)(2,1)} %all-gather.8.cloned.1.call-done), kind=kOutput, calls=%fused_computation.13 | convolution fusion | flops 23630708736 | bytes 74448896 | tf_op jit(solution)/shard_map/lrf,lfd->lrd/dot_general | solution.py:35
  1378.7 18.6 %copy.57 = bf16[1,8,512,2048]{3,1,0,2:T(8,128)(2,1)} copy(bf16[1,8,512,2048]{3,2,1,0:T(8,128)(2,1)} %convert_bitcast_fusion.1) | data formatting | bytes 33554432 | tf_op jit(solution)/shard_map/reshape | solution.py:59
  1397.3 51.2 %all-to-all-done.3 = bf16[1,8,512,2048]{3,1,0,2:T(8,128)(2,1)} async-done(((bf16[1,8,512,2048]{3,1,0,2:T(8,128)(2,1)}), bf16[1,8,512,2048]{3,1,0,2:T(8,128)(2,1)}, u32[]{:S(2)}, u32[]{:S(2)}) %all-to-all-start.3) | async-done | bytes 16777248 | tf_op jit(solution)/shard_map/all_to_all | solution.py:59
  1448.5 6.2 all-to-all-start.1
  1455.7 18.6 %copy.68 = bf16[1,8,8,64,2048]{4,3,1,2,0:T(8,128)(2,1)} copy(bf16[1,8,8,64,2048]{4,1,3,2,0:T(8,128)(2,1)} %bitcast.27) | data formatting | bytes 33554432 | tf_op jit(solution)/shard_map/all_to_all | solution.py:59
  1474.3 31.7 %gather_fusion.3 = bf16[3072,2048]{1,0:T(8,128)(2,1)} fusion(bf16[4096,2048]{1,0:T(8,128)(2,1)} %bitcast.95, s32[3072]{0:T(1024)S(1)} %broadcast_clamp_fusion.2), kind=kCustom, calls=%fused_computation.3.clone | custom fusion | bytes 25178112 | tf_op jit(solution)/shard_map/jit(_take)/gather | solution.py:25
  1506.1 14.3 select_convert_fusion
  1520.4 28.5 %reshape.189 = f32[512,6,2048]{2,1,0:T(8,128)} reshape(f32[3072,2048]{1,0:T(8,128)} %select_convert_fusion) | data formatting | bytes 50331648 | tf_op jit(solution)/shard_map/convert_element_type | solution.py:27
  1548.8 90.1 %all-to-all-done.1 = bf16[1,8,512,2048]{3,1,0,2:T(8,128)(2,1)} async-done(((bf16[1,8,512,2048]{3,1,0,2:T(8,128)(2,1)}), bf16[1,8,512,2048]{3,1,0,2:T(8,128)(2,1)}, u32[]{:S(2)}, u32[]{:S(2)}) %all-to-all-start.1) | async-done | bytes 16777248 | tf_op jit(solution)/shard_map/all_to_all | solution.py:59
  1638.9 18.6 %copy.58 = bf16[1,8,8,64,2048]{4,3,1,2,0:T(8,128)(2,1)} copy(bf16[1,8,8,64,2048]{4,1,3,2,0:T(8,128)(2,1)} %bitcast.11) | data formatting | bytes 33554432 | tf_op jit(solution)/shard_map/all_to_all | solution.py:59
  1657.5 31.7 %gather_fusion.1 = bf16[3072,2048]{1,0:T(8,128)(2,1)} fusion(bf16[4096,2048]{1,0:T(8,128)(2,1)} %bitcast.96, s32[3072]{0:T(1024)S(1)} %broadcast_clamp_fusion.3), kind=kCustom, calls=%fused_computation.1.clone | custom fusion | bytes 25178112 | tf_op jit(solution)/shard_map/jit(_take)/gather | solution.py:25
  1689.2 14.6 select_convert_fusion.1
  1703.8 28.5 %reshape.188 = f32[512,6,2048]{2,1,0:T(8,128)} reshape(f32[3072,2048]{1,0:T(8,128)} %select_convert_fusion.1) | data formatting | bytes 50331648 | tf_op jit(solution)/shard_map/convert_element_type | solution.py:27
  1732.3 20.4 %multiply_reduce_fusion = f32[512,2048]{1,0:T(8,128)} fusion(f32[512,6,2048]{2,1,0:T(8,128)} %reshape.189, f32[512,6]{1,0:T(8,128)S(1)} %bitcast_select_fusion), kind=kLoop, calls=%fused_computation.6 | loop fusion | flops 11534336 | bytes 29372416 | tf_op jit(solution)/shard_map/reduce_sum | solution.py:27
  1752.7 1.5 copy-done
  1754.2 14.4 multiply_reduce_fusion.1
  1768.6 8.3 fusion.1
  (65 shorter events, 5.0 us)
Async XLA Ops:
  6.5 2.4 copy-start.9
  6.5 482.6 %all-gather.4.cloned.1.call-start = ((), (), s32[]{:S(2)}) async-start(), calls=%async_computation.4 | async-start | bytes 57671680 | tf_op jit(solution)/shard_map/all_gather | solution.py:51
  7.3 797.6 %all-gather.6.cloned.1.call-start = ((), (), s32[]{:S(2)}) async-start(), calls=%async_computation.5 | async-start | bytes 57671680 | tf_op jit(solution)/shard_map/all_gather | solution.py:52
  8.1 1195.4 %all-gather.8.cloned.1.call-start = ((), (), s32[]{:S(2)}) async-start(), calls=%async_computation.6 | async-start | bytes 57671680 | tf_op jit(solution)/shard_map/all_gather | solution.py:53
  9.4 32.6 %copy-start.1 = (s32[3072]{0:T(1024)}, s32[3072]{0:T(1024)S(1)}, u32[]{:S(2)}) copy-start(s32[3072]{0:T(1024)S(1)} %eq.58) | copy-start | bytes 36868
  29.6 0.6 copy-start.5
  94.4 190.2 %all-to-all-start.2 = ((bf16[8,8,64,2048]{3,2,1,0:T(8,128)(2,1)}), bf16[8,8,64,2048]{3,2,1,0:T(8,128)(2,1)}, u32[]{:S(2)}, u32[]{:S(2)}) async-start(bf16[8,8,64,2048]{3,2,1,0:T(8,128)(2,1)} %bitcast.97), calls=%async_computation.2 | async-start | bytes 33554432 | tf_op jit(solution)/shard_map/all_to_all | solution.py:57
  100.8 69.4 %copy-start.3 = (s32[3072]{0:T(1024)}, s32[3072]{0:T(1024)S(1)}, u32[]{:S(2)}) copy-start(s32[3072]{0:T(1024)S(1)} %eq.50) | copy-start | bytes 36868
  137.4 32.8 %copy-start.7 = (s32[3072]{0:T(1024)}, s32[3072]{0:T(1024)S(1)}, u32[]{:S(2)}) copy-start(s32[3072]{0:T(1024)S(1)} %fusion.7) | copy-start | bytes 36868
  284.5 190.4 %all-to-all-start = ((bf16[8,8,64,2048]{3,2,1,0:T(8,128)(2,1)}), bf16[8,8,64,2048]{3,2,1,0:T(8,128)(2,1)}, u32[]{:S(2)}, u32[]{:S(2)}) async-start(bf16[8,8,64,2048]{3,2,1,0:T(8,128)(2,1)} %bitcast.98), calls=%async_computation | async-start | bytes 33554432 | tf_op jit(solution)/shard_map/all_to_all | solution.py:57
  1258.1 190.4 %all-to-all-start.3 = ((bf16[1,8,512,2048]{3,1,0,2:T(8,128)(2,1)}), bf16[1,8,512,2048]{3,1,0,2:T(8,128)(2,1)}, u32[]{:S(2)}, u32[]{:S(2)}) async-start(bf16[1,8,512,2048]{3,1,0,2:T(8,128)(2,1)} %copy.67), calls=%async_computation.3 | async-start | bytes 33554432 | tf_op jit(solution)/shard_map/all_to_all | solution.py:59
  1397.3 57.4 %copy-start.2 = (s32[3072]{0:T(1024)S(1)}, s32[3072]{0:T(1024)}, u32[]{:S(2)}) copy-start(s32[3072]{0:T(1024)} %copy-done.1) | copy-start | bytes 36868
  1397.3 57.4 %copy-start.6 = (s32[3072]{0:T(1024)S(1)}, s32[3072]{0:T(1024)}, u32[]{:S(2)}) copy-start(s32[3072]{0:T(1024)} %copy-done.5) | copy-start | bytes 36868
  1397.3 57.7 %copy-start.10 = (f32[2,512,6]{1,0,2:T(2,128)S(1)}, f32[2,512,6]{1,0,2:T(2,128)}, u32[]{:S(2)}) copy-start(f32[2,512,6]{1,0,2:T(2,128)} %param.12) | copy-start | bytes 73732
  1397.3 57.9 %copy-start.4 = (s32[3072]{0:T(1024)S(1)}, s32[3072]{0:T(1024)}, u32[]{:S(2)}) copy-start(s32[3072]{0:T(1024)} %copy-done.3) | copy-start | bytes 36868
  1397.3 57.9 %copy-start.8 = (s32[3072]{0:T(1024)S(1)}, s32[3072]{0:T(1024)}, u32[]{:S(2)}) copy-start(s32[3072]{0:T(1024)} %copy-done.7) | copy-start | bytes 36868
  1448.5 190.5 %all-to-all-start.1 = ((bf16[1,8,512,2048]{3,1,0,2:T(8,128)(2,1)}), bf16[1,8,512,2048]{3,1,0,2:T(8,128)(2,1)}, u32[]{:S(2)}, u32[]{:S(2)}) async-start(bf16[1,8,512,2048]{3,1,0,2:T(8,128)(2,1)} %copy.57), calls=%async_computation.1 | async-start | bytes 33554432 | tf_op jit(solution)/shard_map/all_to_all | solution.py:59
  1732.3 21.9 %copy-start = (f32[512,6,2048]{2,1,0:T(8,128)S(1)}, f32[512,6,2048]{2,1,0:T(8,128)}, u32[]{:S(2)}) copy-start(f32[512,6,2048]{2,1,0:T(8,128)} %reshape.188) | copy-start | bytes 75497472
Sparse Core Ops, SparseCore 0:
  8.9 397.9 all-gather.3
  408.5 396.3 all-gather.5
  806.5 397.0 all-gather.7
where the time goes:
time: 1800 us; the launch traced here: 1780 us
  waiting for transfers between devices  1050 us (58%)
  local copies, waits for them, and re-layouts  313 us (17%)
  matrix products  229 us (13%)
  other arithmetic  155 us (9%)
  starting transfers between devices  24.4 us (1%)
    all_gather x1, waiting for transfers between devices, per_device(): wd_full = lax.all_gather(wd_loc, 'data', axis=2, tiled=True)  361 us
    all_gather x1, waiting for transfers between devices, per_device(): wu_full = lax.all_gather(wu_loc, 'data', axis=1, tiled=True)  275 us
    all_to_all x2, waiting for transfers between devices, per_device(): lax.all_to_all(send_rows.reshape(expert_devs, n_loc, capacity, d_model),...  269 us
    all_to_all x2, waiting for transfers between devices, per_device(): lax.all_to_all(out_rows.reshape(1, n_loc, expert_devs * capacity, d_model...  141 us
    dot_general x2, matrix products, expert_mlp(): jnp.einsum('lrd,ldf->lrf', rows_in, wg_full, preferred_element_type=jnp.f...  81.2 us
    dot_general x2, matrix products, expert_mlp(): jnp.einsum('lrd,ldf->lrf', rows_in, wu_full, preferred_element_type=jnp.f...  76.2 us
    dot_general x2, matrix products, expert_mlp(): jnp.einsum('lrf,lfd->lrd', hidden, wd_full, preferred_element_type=jnp.fl...  71.6 us
    gather x2, local copies, waits for them, and re-layouts, combine_block(): jnp.take(back_rows, jnp.minimum(dest_pos, slot_total - 1), axis=0)  63.5 us
  transfers between devices with their start and end apart: 7, of which 6 were waited for; matrix products, arithmetic and copies ran while one was open for 28% of the time, Pallas kernels for 0%

commit v1 on v0

v1 whole, which is shorter than its diff:
```python
import functools

import jax
import jax.numpy as jnp
from jax import lax
from jax.experimental import pallas as pl
from jax.experimental.pallas import tpu as pltpu
from jax.sharding import PartitionSpec as P

MESH = pl.DeviceIdType.MESH
LANES = 128


def moe_kernel(n_x, cap, x_ref, ids_ref, gate_ref, wg_ref, wu_ref, wd_ref,
               y_ref, xg_ref, rb_ref, bk_ref, lg_ref, lu_ref, ld_ref,
               wg_v, wu_v, wd_v, rows_v, o_v, h_v, acc_v, send_v, ob_v, lt_v, p_v, g_v, pl_v,
               ws, wr, wl, xs, xr, ps, pr, xsem, ssem, rsem, bs, b0, br, br0, osem, ysem):
    n_mb, n_blk, _, d_model = x_ref.shape
    tok = n_blk * cap
    n_loc, d_loc, ff = wg_ref.shape
    half = n_loc // 2
    n_quad = n_blk * 2
    n_exp = n_blk * n_loc
    n_top = ids_ref.shape[1]
    n_tile = 256

    e = lax.axis_index('expert')
    d = lax.axis_index('data')
    x = e // 2
    c = e % 2
    h = d // 2
    twin_d = d + 1 - 2 * (d % 2)
    part_d = 3 - d

    def dev(line, r, cc):
        return {'expert': 2 * ((x + r) % n_x) + (c + cc) % 2, 'data': d + line * (part_d - d)}

    def quad(line, rc):
        r, cc = rc // 2, rc % 2
        return 2 * (2 * ((x + r) % n_x) + (c + cc) % 2) + (h + line * (1 - 2 * h))

    twin = {'expert': e, 'data': twin_d}
    partner = {'expert': e, 'data': part_d}
    self_q = quad(0, 0)

    peers = [dev(line, r, cc) for line in range(2) for r in range(n_x) for cc in range(2) if (line, r, cc) != (0, 0, 0)]
    barrier = pltpu.get_barrier_semaphore()
    for peer in peers + [twin]:
        pl.semaphore_signal(barrier, inc=1, device_id=peer, device_id_type=MESH)
    pl.semaphore_wait(barrier, len(peers) + 1)

    def remote(src, dst, send_sem, recv_sem, device):
        return pltpu.make_async_remote_copy(src_ref=src, dst_ref=dst, send_sem=send_sem, recv_sem=recv_sem,
                                            device_id=device, device_id_type=MESH)

    w_in = (wg_ref, wu_ref, wd_ref)
    w_land = (lg_ref, lu_ref, ld_ref)

    def w_copy(flow, k, a):
        if flow == 0:
            src, device = w_in[a].at[half * h + k], twin
        elif flow == 1:
            src, device = w_in[a].at[half * (1 - h) + k], partner
        else:
            src, device = w_land[a].at[1, k], twin
        return remote(src, w_land[a].at[flow, k], ws.at[flow, k, a], wr.at[flow, k, a], device)

    def w_start(flow, k):
        for a in range(3):
            w_copy(flow, k, a).start()

    def w_forward(k):
        for a in range(3):
            w_copy(1, k, a).wait_recv()
            w_copy(2, k, a).start()

    def x_slot(line, mb, r, cc):
        return xg_ref.at[mb, line * n_blk + r * 2 + cc]

    def x_have(line, mb, r):
        return x_ref.at[mb] if (line, r) == (0, 0) else x_slot(line, mb, r, 0)

    def x_copy(line, mb, r, cc):
        if cc == 1:
            src, device = x_have(line, mb, r), dev(0, 0, 1)
        elif r == 0:
            src, device = x_ref.at[mb], partner
        elif r == n_x - 1:
            src, device = x_have(line, mb, 0), dev(0, 1, 0)
        elif r == 1:
            src, device = x_have(line, mb, 0), dev(0, n_x - 1, 0)
        elif mb == 0:
            src, device = x_have(line, mb, n_x - 1), dev(0, 1, 0)
        else:
            src, device = x_have(line, mb, 1), dev(0, n_x - 1, 0)
        i = line * n_blk + r * 2 + cc
        return remote(src, x_slot(line, mb, r, cc), xs.at[mb, i], xr.at[mb, i], device)

    def x_start(*keys):
        for key in keys:
            x_copy(*key).start()

    def x_wait(*key):
        x_copy(*key).wait_recv()

    def p_copy(line, r, cc):
        rr = (n_x - r) % n_x
        i = line * n_blk + rr * 2 + cc
        return remote(p_v.at[quad(line, r * 2 + cc)], pl_v.at[i], ps.at[i], pr.at[i], dev(line, r, cc))

    w_start(0, 0)
    for mb in range(n_mb):
        x_start((1, mb, 0, 0), (0, mb, 3, 0), (0, mb, 1, 0), (0, mb, 0, 1))

    row_i = lax.broadcasted_iota(jnp.int32, (tok, tok), 0)
    col_i = lax.broadcasted_iota(jnp.int32, (tok, tok), 1)
    earlier = jnp.where(row_i < col_i, 1.0, 0.0).astype(jnp.bfloat16)
    exp_i = lax.broadcasted_iota(jnp.int32, (n_exp, tok), 0)
    for mb in range(n_mb):
        picked = jnp.zeros((n_exp, tok), jnp.float32)
        weight = jnp.zeros((n_exp, tok), jnp.float32)
        for j in range(n_top):
            match = exp_i == ids_ref[mb, j:j + 1, :]
            picked = picked + jnp.where(match, 1.0, 0.0)
            weight = weight + jnp.where(match, gate_ref[mb, j:j + 1, :], 0.0)
        place = jnp.dot(picked.astype(jnp.bfloat16), earlier, preferred_element_type=jnp.float32)
        slot_of = jnp.where(picked > 0.5, jnp.where(place < cap - 0.5, place, -1.0), -1.0)
        p_v[:, mb * half:(mb + 1) * half, :] = slot_of.reshape(n_quad, half, tok)
        g_v[:, mb * half:(mb + 1) * half, :] = weight.reshape(n_quad, half, tok)
    for line in range(2):
        for r in range(n_x):
            for cc in range(2):
                if (line, r, cc) != (0, 0, 0):
                    p_copy(line, r, cc).start()
    w_start(0, 1)
    for k in range(half):
        w_start(1, k)
    pl_v[0] = p_v[self_q]

    for mb in range(n_mb):
        pltpu.make_async_copy(x_ref.at[mb], rows_v.at[mb], xsem.at[mb]).start()
    for mb in range(n_mb):
        pltpu.make_async_copy(x_ref.at[mb], rows_v.at[mb], xsem.at[mb]).wait()
        pltpu.make_async_copy(rows_v.at[mb], x_slot(0, mb, 0, 0), xsem.at[mb]).start()
        acc_v[mb] = rows_v[mb].reshape(tok, d_model).astype(jnp.float32)

    x_wait(0, 0, 3, 0)
    x_start((0, 0, 2, 0), (0, 0, 3, 1))
    x_wait(0, 0, 1, 0)
    x_start((0, 0, 1, 1))
    x_wait(1, 0, 0, 0)
    x_start((1, 0, 3, 0), (1, 0, 1, 0), (1, 0, 0, 1))
    x_wait(0, 1, 3, 0)
    x_start((0, 1, 3, 1))
    x_wait(0, 1, 1, 0)
    x_start((0, 1, 2, 0), (0, 1, 1, 1))
    x_wait(1, 1, 0, 0)
    x_start((1, 1, 3, 0), (1, 1, 1, 0), (1, 1, 0, 1))
    x_wait(0, 0, 2, 0)
    x_start((0, 0, 2, 1))
    x_wait(1, 0, 1, 0)
    x_start((1, 0, 1, 1))
    x_wait(1, 0, 3, 0)
    x_start((1, 0, 2, 0), (1, 0, 3, 1))
    x_wait(0, 1, 2, 0)
    x_start((0, 1, 2, 1))
    w_forward(0)
    w_start(0, 2)
    x_wait(1, 1, 3, 0)
    x_start((1, 1, 3, 1))
    x_wait(1, 1, 1, 0)
    x_start((1, 1, 2, 0), (1, 1, 1, 1))
    x_wait(1, 0, 2, 0)
    x_start((1, 0, 2, 1))
    x_wait(1, 1, 2, 0)
    x_start((1, 1, 2, 1))
    w_forward(1)
    w_start(0, 3)
    for line in range(2):
        for mb in range(n_mb):
            for r in range(n_x):
                x_wait(line, mb, r, 1)
    for line in range(2):
        for r in range(n_x):
            for cc in range(2):
                if (line, r, cc) != (0, 0, 0):
                    p_copy(line, (n_x - r) % n_x, cc).wait_recv()
    for mb in range(n_mb):
        pltpu.make_async_copy(rows_v.at[mb], x_slot(0, mb, 0, 0), xsem.at[mb]).wait()

    n_unit = n_mb * 2 * n_blk
    place_i = lax.broadcasted_iota(jnp.int32, (cap, tok), 0).astype(jnp.float32)

    def x_load(u):
        slot = u % 2
        return pltpu.make_async_copy(xg_ref.at[u // (2 * n_blk), u % (2 * n_blk)], rows_v.at[slot], xsem.at[slot])

    def row_store(u):
        slot = u % 2
        mb, i = u // (2 * n_blk), u % (2 * n_blk)
        return pltpu.make_async_copy(send_v.at[slot], rb_ref.at[pl.ds(0, half), mb, i // n_blk, i % n_blk], ssem.at[slot])

    x_load(0).start()

    def dispatch(u, carry):
        slot = u % 2
        mb, i = u // (2 * n_blk), u % (2 * n_blk)
        x_load(u).wait()

        @pl.when(u + 1 < n_unit)
        def _():
            x_load(u + 1).start()

        pick = jnp.concatenate(
            [jnp.where(pl_v[i, pl.ds(mb * half + k, 1), :] == place_i, 1.0, 0.0) for k in range(half)], axis=0)
        pick = pick.astype(jnp.bfloat16)

        @pl.when(u >= 2)
        def _():
            row_store(u - 2).wait()

        def tile(n, carry):
            cols = pl.ds(pl.multiple_of(n * n_tile, n_tile), n_tile)
            block = rows_v[slot, :, :, cols].reshape(tok, n_tile)
            got = jnp.dot(pick, block, preferred_element_type=jnp.float32).astype(jnp.bfloat16)
            send_v[slot, :, :, cols] = got.reshape(half, cap, n_tile)
            return carry

        lax.fori_loop(0, d_model // n_tile, tile, 0)
        row_store(u).start()
        return carry

    lax.fori_loop(0, n_unit, dispatch, 0)
    row_store(n_unit - 2).wait()
    row_store(n_unit - 1).wait()

    n_chunk = 2 * n_mb
    rows_chunk = n_blk * cap

    def chunk_of(ck):
        return 1 - ck // n_mb, ck % n_mb

    def row_load(k, ck):
        line, mb = chunk_of(ck)
        return pltpu.make_async_copy(rb_ref.at[k, mb, line], rows_v.at[ck % 2], rsem.at[ck % 2])

    def w_load(j, k, a):
        owner = (twin_d, part_d, 3 - twin_d, d)[j]
        at = pl.ds(pl.multiple_of(owner * d_loc, d_loc), d_loc)
        src = w_in[a].at[half * h + k] if j == 3 else w_land[a].at[j, k]
        dst = wd_v.at[:, at] if a == 2 else (wg_v, wu_v)[a].at[at, :]
        return pltpu.make_async_copy(src, dst, wl.at[j, a])

    def far_send(k, ck, rc):
        line, mb = chunk_of(ck)
        r, cc = rc // 2, rc % 2
        back = ((n_x - r) % n_x) * 2 + cc
        return remote(o_v.at[ck, rc], bk_ref.at[k, mb, line, back], bs.at[ck], br.at[k, ck], dev(line, r, cc))

    def near_send(k, ck):
        line, mb = chunk_of(ck)
        return remote(o_v.at[ck, 0], bk_ref.at[k, mb, line, 0], b0.at[ck], br0.at[k, mb], partner)

    def near_copy(k, ck):
        line, mb = chunk_of(ck)
        return pltpu.make_async_copy(o_v.at[ck, 0], bk_ref.at[k, mb, line, 0], b0.at[ck])

    def sent_wait(ck):
        many = o_v.at[ck, pl.ds(1, n_blk - 1)]
        pltpu.make_async_copy(many, many, bs.at[ck]).wait()
        one = o_v.at[ck, 0]
        pltpu.make_async_copy(one, one, b0.at[ck]).wait()

    def compute(k):
        row_load(k, 0).start()
        for a in range(3):
            w_load(3, k, a).start()
        for j in range(3):
            for a in range(3):
                if j != 1:
                    w_copy(j, k, a).wait_recv()
                w_load(j, k, a).start()
        for j in range(4):
            for a in range(3):
                w_load(j, k, a).wait()

        def chunk(ck, carry):
            slot = ck % 2
            row_load(k, ck).wait()

            @pl.when(ck + 1 < n_chunk)
            def _():
                row_load(k, ck + 1).start()

            def up_tile(f, carry):
                cols = pl.ds(pl.multiple_of(f * LANES, LANES), LANES)
                both = jnp.concatenate([wg_v[:, cols], wu_v[:, cols]], axis=1)
                pre = jnp.dot(rows_v[slot].reshape(rows_chunk, d_model), both, preferred_element_type=jnp.float32)
                h_v[:, cols] = (jax.nn.silu(pre[:, :LANES]) * pre[:, LANES:]).astype(jnp.bfloat16)
                return carry

            lax.fori_loop(0, ff // LANES, up_tile, 0)

            @pl.when(k > 0)
            def _():
                sent_wait(ck)

            def down_tile(n, carry):
                cols = pl.ds(pl.multiple_of(n * n_tile, n_tile), n_tile)
                out = jnp.dot(h_v[...], wd_v[:, cols], preferred_element_type=jnp.float32).astype(jnp.bfloat16)
                o_v[ck, :, :, cols] = out.reshape(n_blk, cap, n_tile)
                return carry

            lax.fori_loop(0, d_model // n_tile, down_tile, 0)

            for rc in range(1, n_blk):
                far_send(k, ck, rc).start()

            @pl.when(ck < n_mb)
            def _():
                near_send(k, ck).start()

            @pl.when(ck >= n_mb)
            def _():
                near_copy(k, ck).start()

            return carry

        lax.fori_loop(0, n_chunk, chunk, 0)

    n_grp = n_blk // 4
    k_rows = 4 * cap

    def o_load(k, u):
        line, mb = chunk_of(u // n_grp)
        return pltpu.make_async_copy(bk_ref.at[k, mb, line, pl.ds((u % n_grp) * 4, 4)], ob_v.at[u % 2], osem.at[u % 2])

    def o_ready(k, u):
        ck = u // n_grp
        line, mb = chunk_of(ck)

        @pl.when(u % n_grp == 0)
        def _():
            many = bk_ref.at[k, mb, line, pl.ds(1, n_blk - 1)]
            pltpu.make_async_copy(many, many, br.at[k, ck]).wait()

        @pl.when(jnp.logical_and(u % n_grp == 0, ck < n_mb))
        def _():
            near_send(k, ck).wait_recv()

        o_load(k, u).start()

    def combine(k):
        o_ready(k, 0)

        def unit(u, carry):
            line, mb = chunk_of(u // n_grp)
            slot = u % 2
            parts = []
            for i in range(4):
                q = quad(line, (u % n_grp) * 4 + i)
                hit = p_v[q, pl.ds(mb * half + k, 1), :] == place_i
                parts.append(jnp.where(hit, g_v[q, pl.ds(mb * half + k, 1), :], 0.0))
            mix = jnp.concatenate(parts, axis=0).T
            first = mix.astype(jnp.bfloat16)
            rest = mix - first.astype(jnp.float32)
            second = rest.astype(jnp.bfloat16)
            third = (rest - second.astype(jnp.float32)).astype(jnp.bfloat16)
            lt_v[:, 0:k_rows] = first
            lt_v[:, k_rows:2 * k_rows] = second
            lt_v[:, 2 * k_rows:3 * k_rows] = third
            o_load(k, u).wait()

            @pl.when(u + 1 < n_chunk * n_grp)
            def _():
                o_ready(k, u + 1)

            def tile(n, carry):
                cols = pl.ds(pl.multiple_of(n * n_tile, n_tile), n_tile)
                rows = ob_v[slot, :, :, cols].reshape(k_rows, n_tile)
                acc_v[mb, :, cols] += jnp.dot(lt_v[...], jnp.concatenate([rows, rows, rows], axis=0),
                                              preferred_element_type=jnp.float32)
                return carry

            lax.fori_loop(0, d_model // n_tile, tile, 0)
            return carry

        lax.fori_loop(0, n_chunk * n_grp, unit, 0)

    def step(k, carry):
        @pl.when(k < half)
        def _():
            compute(k)

        @pl.when(k + 2 < half)
        def _():
            w_forward(k + 2)

        @pl.when(k == half)
        def _():
            for ck in range(n_chunk):
                sent_wait(ck)

        @pl.when(k > 0)
        def _():
            combine(k - 1)

        return carry

    lax.fori_loop(0, half + 1, step, 0)

    for mb in range(n_mb):
        rows_v[mb] = acc_v[mb].astype(jnp.bfloat16).reshape(n_blk, cap, d_model)
        pltpu.make_async_copy(rows_v.at[mb], y_ref.at[mb], ysem.at[mb]).start()

    for flow in range(3):
        for k in range(half):
            for a in range(3):
                w_copy(flow, k, a).wait_send()
    for line in range(2):
        for mb in range(n_mb):
            for r in range(n_x):
                for cc in range(2):
                    if (line, r, cc) != (0, 0, 0):
                        x_copy(line, mb, r, cc).wait_send()
    for line in range(2):
        for r in range(n_x):
            for cc in range(2):
                if (line, r, cc) != (0, 0, 0):
                    p_copy(line, r, cc).wait_send()
    for mb in range(n_mb):
        pltpu.make_async_copy(rows_v.at[mb], y_ref.at[mb], ysem.at[mb]).wait()


def solution(mesh):
    expert_devs = mesh.shape['expert']
    n_x = expert_devs // 2
    row_spec = P(None, ('rep', 'expert', 'data'), None)
    up_spec = P('expert', 'data', None)
    down_spec = P('expert', None, 'data')

    def per_device(x_loc, idx_loc, gate_loc, wg_loc, wu_loc, wd_loc):
        n_mb, tok, d_model = x_loc.shape
        n_top = idx_loc.shape[2]
        n_loc, d_loc, ff = wg_loc.shape
        n_exp = n_loc * expert_devs
        half = n_loc // 2
        cap = 8 * ((5 * n_top * tok + 32 * n_exp - 1) // (32 * n_exp))
        assert tok == expert_devs * cap
        bf16, f32 = jnp.bfloat16, jnp.float32
        n_quad = 2 * expert_devs
        rows = (expert_devs, cap, d_model)
        hbm = pl.BlockSpec(memory_space=pl.ANY)
        vmem = pl.BlockSpec(memory_space=pltpu.VMEM)
        dma = pltpu.SemaphoreType.DMA
        out = pl.pallas_call(
            functools.partial(moe_kernel, n_x, cap),
            out_shape=[
                jax.ShapeDtypeStruct((n_mb,) + rows, bf16),
                jax.ShapeDtypeStruct((n_mb, n_quad) + rows, bf16),
                jax.ShapeDtypeStruct((half, n_mb, 2) + rows, bf16),
                jax.ShapeDtypeStruct((half, n_mb, 2) + rows, bf16),
                jax.ShapeDtypeStruct((3, half, d_loc, ff), bf16),
                jax.ShapeDtypeStruct((3, half, d_loc, ff), bf16),
                jax.ShapeDtypeStruct((3, half, ff, d_loc), bf16),
            ],
            in_specs=[hbm, vmem, vmem, hbm, hbm, hbm],
            out_specs=[hbm] * 7,
            scratch_shapes=[
                pltpu.VMEM((4 * d_loc, ff), bf16),
                pltpu.VMEM((4 * d_loc, ff), bf16),
                pltpu.VMEM((ff, 4 * d_loc), bf16),
                pltpu.VMEM((2,) + rows, bf16),
                pltpu.VMEM((2 * n_mb,) + rows, bf16),
                pltpu.VMEM((tok, ff), bf16),
                pltpu.VMEM((n_mb, tok, d_model), f32),
                pltpu.VMEM((2, half, cap, d_model), bf16),
                pltpu.VMEM((2, 4, cap, d_model), bf16),
                pltpu.VMEM((tok, 12 * cap), bf16),
                pltpu.VMEM((n_quad, n_mb * half, tok), f32),
                pltpu.VMEM((n_quad, n_mb * half, tok), f32),
                pltpu.VMEM((n_quad, n_mb * half, tok), f32),
                dma((3, half, 3)), dma((3, half, 3)), dma((4, 3)),
                dma((n_mb, n_quad)), dma((n_mb, n_quad)),
                dma((n_quad,)), dma((n_quad,)),
                dma((2,)), dma((2,)), dma((2,)),
                dma((2 * n_mb,)), dma((2 * n_mb,)),
                dma((half, 2 * n_mb)), dma((half, n_mb)),
                dma((2,)), dma((2,)),
            ],
            compiler_params=pltpu.CompilerParams(collective_id=0, has_side_effects=True, vmem_limit_bytes=62 * 1024 * 1024),
        )(x_loc.reshape((n_mb,) + rows), idx_loc.transpose(0, 2, 1), gate_loc.transpose(0, 2, 1), wg_loc, wu_loc, wd_loc)
        return out[0].reshape(n_mb, tok, d_model)

    return jax.shard_map(per_device, mesh=mesh, in_specs=(row_spec, row_spec, row_spec, up_spec, up_spec, down_spec),
                         out_specs=row_spec, check_vma=False)
```

time: 1800 us -> 955 us (0.53)
  the two profiles are of different devices: /device:TPU:104 before, /device:TPU:118 now
where the time goes in v1:
time: 955 us; the launch traced here: 953 us
  Pallas kernels  945 us (99%)
    pallas_call x1, Pallas kernels, per_device(): pl.pallas_call(functools.partial(moe_kernel, n_x, cap), out_shape=[jax.Sh...  945 us

profile of v1, /device:TPU:118, one launch (start us, length us, event | category | flops | bytes accessed | tf_op | source)
XLA Modules:
  0.0 952.9 jit_solution(7255751743144181961)
XLA Ops:
  0.0 1.4 copy.12
  1.4 1.3 copy.11
  2.7 945.4 %shard_map.64 = (bf16[2,8,64,2048]{3,2,1,0:T(8,128)(2,1)}, bf16[2,16,8,64,2048]{4,3,2,1,0:T(8,128)(2,1)}, bf16[4,2,2,8,64,2048]{5,4,3,2,1,0:T(8,128)(2,1)}, bf16...) custom-call(bf16[2,8,64,2048]{3,2,1,0:T(8,128)(2,1)} %bitcast.8, ...), custom_call_target="tpu_custom_call" | custom-call | tf_op jit(solution)/shard_map/pallas_call | solution.py:456
  948.1 4.8 copy.14

commit v2 on v1

--- a/solution.py
+++ b/solution.py
@@ -21,7 +21,7 @@
     half = n_loc // 2
     n_quad = n_blk * 2
     n_exp = n_blk * n_loc
-    n_top = ids_ref.shape[1]
+    n_top = ids_ref.shape[0]
     n_tile = 256
 
     e = lax.axis_index('expert')
@@ -101,7 +101,8 @@
             x_copy(*key).start()
 
     def x_wait(*key):
-        x_copy(*key).wait_recv()
+        with jax.named_scope('x%d%d%d%d' % key):
+            x_copy(*key).wait_recv()
 
     def p_copy(line, r, cc):
         rr = (n_x - r) % n_x
@@ -120,9 +121,9 @@
         picked = jnp.zeros((n_exp, tok), jnp.float32)
         weight = jnp.zeros((n_exp, tok), jnp.float32)
         for j in range(n_top):
-            match = exp_i == ids_ref[mb, j:j + 1, :]
+            match = exp_i == ids_ref[j, mb:mb + 1, :]
             picked = picked + jnp.where(match, 1.0, 0.0)
-            weight = weight + jnp.where(match, gate_ref[mb, j:j + 1, :], 0.0)
+            weight = weight + jnp.where(match, gate_ref[j, mb:mb + 1, :], 0.0)
         place = jnp.dot(picked.astype(jnp.bfloat16), earlier, preferred_element_type=jnp.float32)
         slot_of = jnp.where(picked > 0.5, jnp.where(place < cap - 0.5, place, -1.0), -1.0)
         p_v[:, mb * half:(mb + 1) * half, :] = slot_of.reshape(n_quad, half, tok)
@@ -164,8 +165,8 @@
     x_start((1, 0, 2, 0), (1, 0, 3, 1))
     x_wait(0, 1, 2, 0)
     x_start((0, 1, 2, 1))
-    w_forward(0)
-    w_start(0, 2)
+    with jax.named_scope('fwd0'):
+        w_forward(0)
     x_wait(1, 1, 3, 0)
     x_start((1, 1, 3, 1))
     x_wait(1, 1, 1, 0)
@@ -174,8 +175,9 @@
     x_start((1, 0, 2, 1))
     x_wait(1, 1, 2, 0)
     x_start((1, 1, 2, 1))
-    w_forward(1)
-    w_start(0, 3)
+    with jax.named_scope('fwd1'):
+        w_forward(1)
+    w_start(0, 2)
     for line in range(2):
         for mb in range(n_mb):
             for r in range(n_x):
@@ -230,7 +232,8 @@
         row_store(u).start()
         return carry
 
-    lax.fori_loop(0, n_unit, dispatch, 0)
+    with jax.named_scope('dispatch'):
+        lax.fori_loop(0, n_unit, dispatch, 0)
     row_store(n_unit - 2).wait()
     row_store(n_unit - 1).wait()
 
@@ -275,16 +278,21 @@
         row_load(k, 0).start()
         for a in range(3):
             w_load(3, k, a).start()
-        for j in range(3):
+        for a in range(3):
+            w_load(1, k, a).start()
+        with jax.named_scope('wait_own'):
             for a in range(3):
-                if j != 1:
-                    w_copy(j, k, a).wait_recv()
-                w_load(j, k, a).start()
-        for j in range(4):
-            for a in range(3):
-                w_load(j, k, a).wait()
-
-        def chunk(ck, carry):
+                w_copy(0, k, a).wait_recv()
+                w_load(0, k, a).start()
+        with jax.named_scope('wait_up'):
+            for a in range(2):
+                w_copy(2, k, a).wait_recv()
+                w_load(2, k, a).start()
+            for j in range(4):
+                for a in range(2):
+                    w_load(j, k, a).wait()
+
+        def up_chunk(ck, carry):
             slot = ck % 2
             row_load(k, ck).wait()
 
@@ -296,25 +304,33 @@
                 cols = pl.ds(pl.multiple_of(f * LANES, LANES), LANES)
                 both = jnp.concatenate([wg_v[:, cols], wu_v[:, cols]], axis=1)
                 pre = jnp.dot(rows_v[slot].reshape(rows_chunk, d_model), both, preferred_element_type=jnp.float32)
-                h_v[:, cols] = (jax.nn.silu(pre[:, :LANES]) * pre[:, LANES:]).astype(jnp.bfloat16)
+                h_v[ck, :, cols] = (jax.nn.silu(pre[:, :LANES]) * pre[:, LANES:]).astype(jnp.bfloat16)
                 return carry
 
             lax.fori_loop(0, ff // LANES, up_tile, 0)
-
+            return carry
+
+        with jax.named_scope('up'):
+            lax.fori_loop(0, n_chunk, up_chunk, 0)
+        with jax.named_scope('wait_down'):
+            w_copy(2, k, 2).wait_recv()
+            w_load(2, k, 2).start()
+            for j in range(4):
+                w_load(j, k, 2).wait()
+
+        def down_chunk(ck, carry):
             @pl.when(k > 0)
             def _():
-                sent_wait(ck)
+                with jax.named_scope('wait_sent'):
+                    sent_wait(ck)
 
             def down_tile(n, carry):
                 cols = pl.ds(pl.multiple_of(n * n_tile, n_tile), n_tile)
-                out = jnp.dot(h_v[...], wd_v[:, cols], preferred_element_type=jnp.float32).astype(jnp.bfloat16)
+                out = jnp.dot(h_v[ck], wd_v[:, cols], preferred_element_type=jnp.float32).astype(jnp.bfloat16)
                 o_v[ck, :, :, cols] = out.reshape(n_blk, cap, n_tile)
                 return carry
 
             lax.fori_loop(0, d_model // n_tile, down_tile, 0)
-
-            for rc in range(1, n_blk):
-                far_send(k, ck, rc).start()
 
             @pl.when(ck < n_mb)
             def _():
@@ -324,29 +340,38 @@
             def _():
                 near_copy(k, ck).start()
 
+            for rc in range(1, n_blk):
+                far_send(k, ck, rc).start()
             return carry
 
-        lax.fori_loop(0, n_chunk, chunk, 0)
+        with jax.named_scope('down'):
+            lax.fori_loop(0, n_chunk, down_chunk, 0)
 
     n_grp = n_blk // 4
     k_rows = 4 * cap
 
+    def mix_of(u):
+        v = u // n_grp
+        return v % 2, v // 2
+
     def o_load(k, u):
-        line, mb = chunk_of(u // n_grp)
+        line, mb = mix_of(u)
         return pltpu.make_async_copy(bk_ref.at[k, mb, line, pl.ds((u % n_grp) * 4, 4)], ob_v.at[u % 2], osem.at[u % 2])
 
     def o_ready(k, u):
-        ck = u // n_grp
-        line, mb = chunk_of(ck)
+        line, mb = mix_of(u)
+        ck = (1 - line) * n_mb + mb
 
         @pl.when(u % n_grp == 0)
         def _():
-            many = bk_ref.at[k, mb, line, pl.ds(1, n_blk - 1)]
-            pltpu.make_async_copy(many, many, br.at[k, ck]).wait()
-
-        @pl.when(jnp.logical_and(u % n_grp == 0, ck < n_mb))
-        def _():
-            near_send(k, ck).wait_recv()
+            with jax.named_scope('wait_back'):
+                many = bk_ref.at[k, mb, line, pl.ds(1, n_blk - 1)]
+                pltpu.make_async_copy(many, many, br.at[k, ck]).wait()
+
+        @pl.when(jnp.logical_and(u % n_grp == 0, line == 1))
+        def _():
+            with jax.named_scope('wait_near'):
+                near_send(k, ck).wait_recv()
 
         o_load(k, u).start()
 
@@ -354,7 +379,7 @@
         o_ready(k, 0)
 
         def unit(u, carry):
-            line, mb = chunk_of(u // n_grp)
+            line, mb = mix_of(u)
             slot = u % 2
             parts = []
             for i in range(4):
@@ -394,16 +419,23 @@
 
         @pl.when(k + 2 < half)
         def _():
-            w_forward(k + 2)
+            with jax.named_scope('fwd'):
+                w_forward(k + 2)
+
+        @pl.when(k + 3 < half)
+        def _():
+            w_start(0, k + 3)
 
         @pl.when(k == half)
         def _():
-            for ck in range(n_chunk):
-                sent_wait(ck)
+            with jax.named_scope('sent_last'):
+                for ck in range(n_chunk):
+                    sent_wait(ck)
 
         @pl.when(k > 0)
         def _():
-            combine(k - 1)
+            with jax.named_scope('combine'):
+                combine(k - 1)
 
         return carry
 
@@ -413,10 +445,11 @@
         rows_v[mb] = acc_v[mb].astype(jnp.bfloat16).reshape(n_blk, cap, d_model)
         pltpu.make_async_copy(rows_v.at[mb], y_ref.at[mb], ysem.at[mb]).start()
 
-    for flow in range(3):
-        for k in range(half):
-            for a in range(3):
-                w_copy(flow, k, a).wait_send()
+    with jax.named_scope('drain'):
+        for flow in range(3):
+            for k in range(half):
+                for a in range(3):
+                    w_copy(flow, k, a).wait_send()
     for line in range(2):
         for mb in range(n_mb):
             for r in range(n_x):
@@ -472,7 +505,7 @@
                 pltpu.VMEM((ff, 4 * d_loc), bf16),
                 pltpu.VMEM((2,) + rows, bf16),
                 pltpu.VMEM((2 * n_mb,) + rows, bf16),
-                pltpu.VMEM((tok, ff), bf16),
+                pltpu.VMEM((2 * n_mb, tok, ff), bf16),
                 pltpu.VMEM((n_mb, tok, d_model), f32),
                 pltpu.VMEM((2, half, cap, d_model), bf16),
                 pltpu.VMEM((2, 4, cap, d_model), bf16),
@@ -489,7 +522,7 @@
                 dma((2,)), dma((2,)),
             ],
             compiler_params=pltpu.CompilerParams(collective_id=0, has_side_effects=True, vmem_limit_bytes=62 * 1024 * 1024),
-        )(x_loc.reshape((n_mb,) + rows), idx_loc.transpose(0, 2, 1), gate_loc.transpose(0, 2, 1), wg_loc, wu_loc, wd_loc)
+        )(x_loc.reshape((n_mb,) + rows), idx_loc.transpose(2, 0, 1), gate_loc.transpose(2, 0, 1), wg_loc, wu_loc, wd_loc)
         return out[0].reshape(n_mb, tok, d_model)
 
     return jax.shard_map(per_device, mesh=mesh, in_specs=(row_spec, row_spec, row_spec, up_spec, up_spec, down_spec),

time: 955 us -> 938 us (0.982)
  the two profiles are of different devices: /device:TPU:118 before, /device:TPU:104 now
where the time goes in v2:
time: 938 us; the launch traced here: 922 us
  Pallas kernels  917 us (98%)
    pallas_call x1, Pallas kernels, per_device(): pl.pallas_call(functools.partial(moe_kernel, n_x, cap), out_shape=[jax.Sh...  917 us

profile of v2, /device:TPU:104, one launch (start us, length us, event | category | flops | bytes accessed | tf_op | source)
XLA Modules:
  0.0 921.6 jit_solution(6887643746535075040)
XLA Ops:
  0.0 916.8 %shard_map.64 = (bf16[2,8,64,2048]{3,2,1,0:T(8,128)(2,1)}, bf16[2,16,8,64,2048]{4,3,2,1,0:T(8,128)(2,1)}, bf16[4,2,2,8,64,2048]{5,4,3,2,1,0:T(8,128)(2,1)}, bf16...) custom-call(bf16[2,8,64,2048]{3,2,1,0:T(8,128)(2,1)} %bitcast.4, ...), custom_call_target="tpu_custom_call" | custom-call | tf_op jit(solution)/shard_map/pallas_call | solution.py:489
  916.9 4.8 copy.8

commit v3 on v1

--- a/solution.py
+++ b/solution.py
@@ -21,8 +21,9 @@
     half = n_loc // 2
     n_quad = n_blk * 2
     n_exp = n_blk * n_loc
-    n_top = ids_ref.shape[1]
-    n_tile = 256
+    n_top = ids_ref.shape[0]
+    n_tile = min(256, d_loc)
+    n_part = d_loc // n_tile
 
     e = lax.axis_index('expert')
     d = lax.axis_index('data')
@@ -120,9 +121,9 @@
         picked = jnp.zeros((n_exp, tok), jnp.float32)
         weight = jnp.zeros((n_exp, tok), jnp.float32)
         for j in range(n_top):
-            match = exp_i == ids_ref[mb, j:j + 1, :]
+            match = exp_i == ids_ref[j, mb:mb + 1, :]
             picked = picked + jnp.where(match, 1.0, 0.0)
-            weight = weight + jnp.where(match, gate_ref[mb, j:j + 1, :], 0.0)
+            weight = weight + jnp.where(match, gate_ref[j, mb:mb + 1, :], 0.0)
         place = jnp.dot(picked.astype(jnp.bfloat16), earlier, preferred_element_type=jnp.float32)
         slot_of = jnp.where(picked > 0.5, jnp.where(place < cap - 0.5, place, -1.0), -1.0)
         p_v[:, mb * half:(mb + 1) * half, :] = slot_of.reshape(n_quad, half, tok)
@@ -132,7 +133,8 @@
             for cc in range(2):
                 if (line, r, cc) != (0, 0, 0):
                     p_copy(line, r, cc).start()
-    w_start(0, 1)
+    for k in range(1, half - 1):
+        w_start(0, k)
     for k in range(half):
         w_start(1, k)
     pl_v[0] = p_v[self_q]
@@ -165,7 +167,6 @@
     x_wait(0, 1, 2, 0)
     x_start((0, 1, 2, 1))
     w_forward(0)
-    w_start(0, 2)
     x_wait(1, 1, 3, 0)
     x_start((1, 1, 3, 1))
     x_wait(1, 1, 1, 0)
@@ -175,7 +176,6 @@
     x_wait(1, 1, 2, 0)
     x_start((1, 1, 2, 1))
     w_forward(1)
-    w_start(0, 3)
     for line in range(2):
         for mb in range(n_mb):
             for r in range(n_x):
@@ -248,22 +248,27 @@
         owner = (twin_d, part_d, 3 - twin_d, d)[j]
         at = pl.ds(pl.multiple_of(owner * d_loc, d_loc), d_loc)
         src = w_in[a].at[half * h + k] if j == 3 else w_land[a].at[j, k]
-        dst = wd_v.at[:, at] if a == 2 else (wg_v, wu_v)[a].at[at, :]
+        dst = wd_v.at[(j + 1) % 4] if a == 2 else (wg_v, wu_v)[a].at[at, :]
         return pltpu.make_async_copy(src, dst, wl.at[j, a])
 
-    def far_send(k, ck, rc):
+    first, last = pl.ds(0, 3), pl.ds(3, 1)
+
+    def send(k, ck, cols):
         line, mb = chunk_of(ck)
-        r, cc = rc // 2, rc % 2
-        back = ((n_x - r) % n_x) * 2 + cc
-        return remote(o_v.at[ck, rc], bk_ref.at[k, mb, line, back], bs.at[ck], br.at[k, ck], dev(line, r, cc))
-
-    def near_send(k, ck):
-        line, mb = chunk_of(ck)
-        return remote(o_v.at[ck, 0], bk_ref.at[k, mb, line, 0], b0.at[ck], br0.at[k, mb], partner)
-
-    def near_copy(k, ck):
-        line, mb = chunk_of(ck)
-        return pltpu.make_async_copy(o_v.at[ck, 0], bk_ref.at[k, mb, line, 0], b0.at[ck])
+
+        @pl.when(line == 1)
+        def _():
+            remote(o_v.at[ck, 0, cols], bk_ref.at[k, mb, 1, 0, cols], b0.at[ck], br0.at[k, mb], partner).start()
+
+        @pl.when(line == 0)
+        def _():
+            pltpu.make_async_copy(o_v.at[ck, 0, cols], bk_ref.at[k, mb, 0, 0, cols], b0.at[ck]).start()
+
+        for rc in range(1, n_blk):
+            r, cc = rc // 2, rc % 2
+            back = ((n_x - r) % n_x) * 2 + cc
+            remote(o_v.at[ck, rc, cols], bk_ref.at[k, mb, line, back, cols], bs.at[ck], br.at[k, ck],
+                   dev(line, r, cc)).start()
 
     def sent_wait(ck):
         many = o_v.at[ck, pl.ds(1, n_blk - 1)]
@@ -271,20 +276,33 @@
         one = o_v.at[ck, 0]
         pltpu.make_async_copy(one, one, b0.at[ck]).wait()
 
+    def down(ck, begin, end):
+        def tile(n, carry):
+            part = n // n_part
+            cols = pl.ds(pl.multiple_of((n % n_part) * n_tile, n_tile), n_tile)
+            out = jnp.dot(h_v[ck], wd_v[part, :, cols], preferred_element_type=jnp.float32).astype(jnp.bfloat16)
+            o_v[ck, :, part, :, cols] = out.reshape(n_blk, cap, n_tile)
+            return carry
+
+        lax.fori_loop(begin * n_part, end * n_part, tile, 0)
+
     def compute(k):
         row_load(k, 0).start()
         for a in range(3):
             w_load(3, k, a).start()
-        for j in range(3):
-            for a in range(3):
-                if j != 1:
-                    w_copy(j, k, a).wait_recv()
-                w_load(j, k, a).start()
+        for a in range(3):
+            w_load(1, k, a).start()
+        for a in range(3):
+            w_copy(0, k, a).wait_recv()
+            w_load(0, k, a).start()
+        for a in range(2):
+            w_copy(2, k, a).wait_recv()
+            w_load(2, k, a).start()
         for j in range(4):
-            for a in range(3):
+            for a in range(2):
                 w_load(j, k, a).wait()
 
-        def chunk(ck, carry):
+        def up_chunk(ck, carry):
             slot = ck % 2
             row_load(k, ck).wait()
 
@@ -296,7 +314,7 @@
                 cols = pl.ds(pl.multiple_of(f * LANES, LANES), LANES)
                 both = jnp.concatenate([wg_v[:, cols], wu_v[:, cols]], axis=1)
                 pre = jnp.dot(rows_v[slot].reshape(rows_chunk, d_model), both, preferred_element_type=jnp.float32)
-                h_v[:, cols] = (jax.nn.silu(pre[:, :LANES]) * pre[:, LANES:]).astype(jnp.bfloat16)
+                h_v[ck, :, cols] = (jax.nn.silu(pre[:, :LANES]) * pre[:, LANES:]).astype(jnp.bfloat16)
                 return carry
 
             lax.fori_loop(0, ff // LANES, up_tile, 0)
@@ -305,48 +323,48 @@
             def _():
                 sent_wait(ck)
 
-            def down_tile(n, carry):
-                cols = pl.ds(pl.multiple_of(n * n_tile, n_tile), n_tile)
-                out = jnp.dot(h_v[...], wd_v[:, cols], preferred_element_type=jnp.float32).astype(jnp.bfloat16)
-                o_v[ck, :, :, cols] = out.reshape(n_blk, cap, n_tile)
-                return carry
-
-            lax.fori_loop(0, d_model // n_tile, down_tile, 0)
-
-            for rc in range(1, n_blk):
-                far_send(k, ck, rc).start()
-
-            @pl.when(ck < n_mb)
-            def _():
-                near_send(k, ck).start()
-
-            @pl.when(ck >= n_mb)
-            def _():
-                near_copy(k, ck).start()
-
+            down(ck, 0, 3)
+            send(k, ck, first)
             return carry
 
-        lax.fori_loop(0, n_chunk, chunk, 0)
+        for j in (3, 0, 1):
+            w_load(j, k, 2).wait()
+        lax.fori_loop(0, n_chunk, up_chunk, 0)
+        w_copy(2, k, 2).wait_recv()
+        w_load(2, k, 2).start()
+        w_load(2, k, 2).wait()
+
+        def down_chunk(ck, carry):
+            down(ck, 3, 4)
+            send(k, ck, last)
+            return carry
+
+        lax.fori_loop(0, n_chunk, down_chunk, 0)
 
     n_grp = n_blk // 4
     k_rows = 4 * cap
 
+    def mix_of(u):
+        v = u // n_grp
+        return v % 2, v // 2
+
     def o_load(k, u):
-        line, mb = chunk_of(u // n_grp)
+        line, mb = mix_of(u)
         return pltpu.make_async_copy(bk_ref.at[k, mb, line, pl.ds((u % n_grp) * 4, 4)], ob_v.at[u % 2], osem.at[u % 2])
 
     def o_ready(k, u):
-        ck = u // n_grp
-        line, mb = chunk_of(ck)
+        line, mb = mix_of(u)
+        ck = (1 - line) * n_mb + mb
 
         @pl.when(u % n_grp == 0)
         def _():
             many = bk_ref.at[k, mb, line, pl.ds(1, n_blk - 1)]
             pltpu.make_async_copy(many, many, br.at[k, ck]).wait()
 
-        @pl.when(jnp.logical_and(u % n_grp == 0, ck < n_mb))
-        def _():
-            near_send(k, ck).wait_recv()
+        @pl.when(jnp.logical_and(u % n_grp == 0, line == 1))
+        def _():
+            one = bk_ref.at[k, mb, line, 0]
+            pltpu.make_async_copy(one, one, br0.at[k, mb]).wait()
 
         o_load(k, u).start()
 
@@ -354,7 +372,7 @@
         o_ready(k, 0)
 
         def unit(u, carry):
-            line, mb = chunk_of(u // n_grp)
+            line, mb = mix_of(u)
             slot = u % 2
             parts = []
             for i in range(4):
@@ -371,18 +389,34 @@
             lt_v[:, 2 * k_rows:3 * k_rows] = third
             o_load(k, u).wait()
 
-            @pl.when(u + 1 < n_chunk * n_grp)
+            @pl.when((u + 1) % n_grp != 0)
             def _():
                 o_ready(k, u + 1)
 
+            d_src = d + line * (3 - 2 * d)
+
             def tile(n, carry):
-                cols = pl.ds(pl.multiple_of(n * n_tile, n_tile), n_tile)
-                rows = ob_v[slot, :, :, cols].reshape(k_rows, n_tile)
-                acc_v[mb, :, cols] += jnp.dot(lt_v[...], jnp.concatenate([rows, rows, rows], axis=0),
+                part = n // n_part
+                owner = d_src + (part % 2) * (1 - 2 * (d_src % 2))
+                owner = owner + (part // 2) * (3 - 2 * owner)
+                cols = pl.ds(pl.multiple_of((n % n_part) * n_tile, n_tile), n_tile)
+                rows = ob_v[slot, :, part, :, cols].reshape(k_rows, n_tile)
+                at = pl.ds(pl.multiple_of(owner * d_loc + (n % n_part) * n_tile, n_tile), n_tile)
+                acc_v[mb, :, at] += jnp.dot(lt_v[...], jnp.concatenate([rows, rows, rows], axis=0),
                                               preferred_element_type=jnp.float32)
                 return carry
 
             lax.fori_loop(0, d_model // n_tile, tile, 0)
+
+            @pl.when(jnp.logical_and((u + 1) % n_grp == 0, u + 1 < n_chunk * n_grp))
+            def _():
+                o_ready(k, u + 1)
+
+            @pl.when(jnp.logical_and(k == half - 1, (u + 1) % (2 * n_grp) == 0))
+            def _():
+                rows_v[mb] = acc_v[mb].astype(jnp.bfloat16).reshape(n_blk, cap, d_model)
+                pltpu.make_async_copy(rows_v.at[mb], y_ref.at[mb], ysem.at[mb]).start()
+
             return carry
 
         lax.fori_loop(0, n_chunk * n_grp, unit, 0)
@@ -396,6 +430,10 @@
         def _():
             w_forward(k + 2)
 
+        @pl.when(k == 0)
+        def _():
+            w_start(0, half - 1)
+
         @pl.when(k == half)
         def _():
             for ck in range(n_chunk):
@@ -408,10 +446,6 @@
         return carry
 
     lax.fori_loop(0, half + 1, step, 0)
-
-    for mb in range(n_mb):
-        rows_v[mb] = acc_v[mb].astype(jnp.bfloat16).reshape(n_blk, cap, d_model)
-        pltpu.make_async_copy(rows_v.at[mb], y_ref.at[mb], ysem.at[mb]).start()
 
     for flow in range(3):
         for k in range(half):
@@ -450,6 +484,7 @@
         bf16, f32 = jnp.bfloat16, jnp.float32
         n_quad = 2 * expert_devs
         rows = (expert_devs, cap, d_model)
+        shards = (expert_devs, 4, cap, d_loc)
         hbm = pl.BlockSpec(memory_space=pl.ANY)
         vmem = pl.BlockSpec(memory_space=pltpu.VMEM)
         dma = pltpu.SemaphoreType.DMA
@@ -459,7 +494,7 @@
                 jax.ShapeDtypeStruct((n_mb,) + rows, bf16),
                 jax.ShapeDtypeStruct((n_mb, n_quad) + rows, bf16),
                 jax.ShapeDtypeStruct((half, n_mb, 2) + rows, bf16),
-                jax.ShapeDtypeStruct((half, n_mb, 2) + rows, bf16),
+                jax.ShapeDtypeStruct((half, n_mb, 2) + shards, bf16),
                 jax.ShapeDtypeStruct((3, half, d_loc, ff), bf16),
                 jax.ShapeDtypeStruct((3, half, d_loc, ff), bf16),
                 jax.ShapeDtypeStruct((3, half, ff, d_loc), bf16),
@@ -469,13 +504,13 @@
             scratch_shapes=[
                 pltpu.VMEM((4 * d_loc, ff), bf16),
                 pltpu.VMEM((4 * d_loc, ff), bf16),
-                pltpu.VMEM((ff, 4 * d_loc), bf16),
+                pltpu.VMEM((4, ff, d_loc), bf16),
                 pltpu.VMEM((2,) + rows, bf16),
-                pltpu.VMEM((2 * n_mb,) + rows, bf16),
-                pltpu.VMEM((tok, ff), bf16),
+                pltpu.VMEM((2 * n_mb,) + shards, bf16),
+                pltpu.VMEM((2 * n_mb, tok, ff), bf16),
                 pltpu.VMEM((n_mb, tok, d_model), f32),
                 pltpu.VMEM((2, half, cap, d_model), bf16),
-                pltpu.VMEM((2, 4, cap, d_model), bf16),
+                pltpu.VMEM((2, 4, 4, cap, d_loc), bf16),
                 pltpu.VMEM((tok, 12 * cap), bf16),
                 pltpu.VMEM((n_quad, n_mb * half, tok), f32),
                 pltpu.VMEM((n_quad, n_mb * half, tok), f32),
@@ -489,7 +524,7 @@
                 dma((2,)), dma((2,)),
             ],
             compiler_params=pltpu.CompilerParams(collective_id=0, has_side_effects=True, vmem_limit_bytes=62 * 1024 * 1024),
-        )(x_loc.reshape((n_mb,) + rows), idx_loc.transpose(0, 2, 1), gate_loc.transpose(0, 2, 1), wg_loc, wu_loc, wd_loc)
+        )(x_loc.reshape((n_mb,) + rows), idx_loc.transpose(2, 0, 1), gate_loc.transpose(2, 0, 1), wg_loc, wu_loc, wd_loc)
         return out[0].reshape(n_mb, tok, d_model)
 
     return jax.shard_map(per_device, mesh=mesh, in_specs=(row_spec, row_spec, row_spec, up_spec, up_spec, down_spec),

time: 955 us -> 927 us (0.971)
  the two profiles are of different devices: /device:TPU:118 before, /device:TPU:104 now
where the time goes in v3:
time: 927 us; the launch traced here: 925 us
  Pallas kernels  920 us (99%)
    pallas_call x1, Pallas kernels, per_device(): pl.pallas_call(functools.partial(moe_kernel, n_x, cap), out_shape=[jax.Sh...  920 us

profile of v3, /device:TPU:104, one launch (start us, length us, event | category | flops | bytes accessed | tf_op | source)
XLA Modules:
  0.0 925.0 jit_solution(6757788351744757482)
XLA Ops:
  0.0 920.2 %shard_map.64 = (bf16[2,8,64,2048]{3,2,1,0:T(8,128)(2,1)}, bf16[2,16,8,64,2048]{4,3,2,1,0:T(8,128)(2,1)}, bf16[4,2,2,8,64,2048]{5,4,3,2,1,0:T(8,128)(2,1)}, bf16...) custom-call(bf16[2,8,64,2048]{3,2,1,0:T(8,128)(2,1)} %bitcast.4, ...), custom_call_target="tpu_custom_call" | custom-call | tf_op jit(solution)/shard_map/pallas_call | solution.py:491
  920.2 4.8 copy.8

commit v4 on v3

--- a/solution.py
+++ b/solution.py
@@ -12,9 +12,9 @@
 
 
 def moe_kernel(n_x, cap, x_ref, ids_ref, gate_ref, wg_ref, wu_ref, wd_ref,
-               y_ref, xg_ref, rb_ref, bk_ref, lg_ref, lu_ref, ld_ref,
+               y_ref, xg_ref, rb_ref, bk_ref, st_ref, lg_ref, lu_ref, ld_ref,
                wg_v, wu_v, wd_v, rows_v, o_v, h_v, acc_v, send_v, ob_v, lt_v, p_v, g_v, pl_v,
-               ws, wr, wl, xs, xr, ps, pr, xsem, ssem, rsem, bs, b0, br, br0, osem, ysem):
+               ws, wr, wl, xs, xr, ps, pr, xsem, ssem, rsem, bs, b0, br, br0, fr, fs, osem, ysem):
     n_mb, n_blk, _, d_model = x_ref.shape
     tok = n_blk * cap
     n_loc, d_loc, ff = wg_ref.shape
@@ -264,11 +264,29 @@
         def _():
             pltpu.make_async_copy(o_v.at[ck, 0, cols], bk_ref.at[k, mb, 0, 0, cols], b0.at[ck]).start()
 
+        @pl.when(line == 1)
+        def _():
+            relay(k, mb, cols).start()
+
+        @pl.when(line == 0)
+        def _():
+            for rc in range(1, n_blk):
+                remote(o_v.at[ck, rc, cols], bk_ref.at[k, mb, 0, back_of(rc), cols], bs.at[ck], br.at[k, ck],
+                       dev(0, rc // 2, rc % 2)).start()
+
+    def back_of(rc):
+        return ((n_x - rc // 2) % n_x) * 2 + rc % 2
+
+    def relay(k, mb, cols):
+        phase = 0 if cols is first else 1
+        return remote(o_v.at[mb, pl.ds(1, n_blk - 1), cols], st_ref.at[k, mb, pl.ds(0, n_blk - 1), cols], bs.at[mb],
+                      fr.at[k, mb, phase], partner)
+
+    def relay_on(k, mb, cols):
+        relay(k, mb, cols).wait_recv()
         for rc in range(1, n_blk):
-            r, cc = rc // 2, rc % 2
-            back = ((n_x - r) % n_x) * 2 + cc
-            remote(o_v.at[ck, rc, cols], bk_ref.at[k, mb, line, back, cols], bs.at[ck], br.at[k, ck],
-                   dev(line, r, cc)).start()
+            remote(st_ref.at[k, mb, rc - 1, cols], bk_ref.at[k, mb, 1, back_of(rc), cols], fs.at[k, mb], br.at[k, mb],
+                   dev(0, rc // 2, rc % 2)).start()
 
     def sent_wait(ck):
         many = o_v.at[ck, pl.ds(1, n_blk - 1)]
@@ -285,6 +303,12 @@
             return carry
 
         lax.fori_loop(begin * n_part, end * n_part, tile, 0)
+
+    def relay_rest(k):
+        for mb in range(1, n_mb):
+            relay_on(k, mb, first)
+        for mb in range(n_mb):
+            relay_on(k, mb, last)
 
     def compute(k):
         row_load(k, 0).start()
@@ -295,6 +319,11 @@
         for a in range(3):
             w_copy(0, k, a).wait_recv()
             w_load(0, k, a).start()
+
+        @pl.when(k > 0)
+        def _():
+            relay_on(k - 1, 0, first)
+
         for a in range(2):
             w_copy(2, k, a).wait_recv()
             w_load(2, k, a).start()
@@ -330,6 +359,11 @@
         for j in (3, 0, 1):
             w_load(j, k, 2).wait()
         lax.fori_loop(0, n_chunk, up_chunk, 0)
+
+        @pl.when(k > 0)
+        def _():
+            relay_rest(k - 1)
+
         w_copy(2, k, 2).wait_recv()
         w_load(2, k, 2).start()
         w_load(2, k, 2).wait()
@@ -346,7 +380,7 @@
 
     def mix_of(u):
         v = u // n_grp
-        return v % 2, v // 2
+        return v // n_mb, v % n_mb
 
     def o_load(k, u):
         line, mb = mix_of(u)
@@ -369,6 +403,10 @@
         o_load(k, u).start()
 
     def combine(k):
+        @pl.when(k == half - 1)
+        def _():
+            relay_on(k, 0, first)
+
         o_ready(k, 0)
 
         def unit(u, carry):
@@ -408,15 +446,19 @@
 
             lax.fori_loop(0, d_model // n_tile, tile, 0)
 
+            @pl.when(jnp.logical_and(k == half - 1, jnp.logical_and(line == 1, (u + 1) % n_grp == 0)))
+            def _():
+                rows_v[mb] = acc_v[mb].astype(jnp.bfloat16).reshape(n_blk, cap, d_model)
+                pltpu.make_async_copy(rows_v.at[mb], y_ref.at[mb], ysem.at[mb]).start()
+
+            @pl.when(jnp.logical_and(k == half - 1, u + 1 == n_mb * n_grp))
+            def _():
+                relay_rest(k)
+
             @pl.when(jnp.logical_and((u + 1) % n_grp == 0, u + 1 < n_chunk * n_grp))
             def _():
                 o_ready(k, u + 1)
 
-            @pl.when(jnp.logical_and(k == half - 1, (u + 1) % (2 * n_grp) == 0))
-            def _():
-                rows_v[mb] = acc_v[mb].astype(jnp.bfloat16).reshape(n_blk, cap, d_model)
-                pltpu.make_async_copy(rows_v.at[mb], y_ref.at[mb], ysem.at[mb]).start()
-
             return carry
 
         lax.fori_loop(0, n_chunk * n_grp, unit, 0)
@@ -447,6 +489,10 @@
 
     lax.fori_loop(0, half + 1, step, 0)
 
+    for k in range(half):
+        for mb in range(n_mb):
+            many = st_ref.at[k, mb]
+            pltpu.make_async_copy(many, many, fs.at[k, mb]).wait()
     for flow in range(3):
         for k in range(half):
             for a in range(3):
@@ -495,12 +541,13 @@
                 jax.ShapeDtypeStruct((n_mb, n_quad) + rows, bf16),
                 jax.ShapeDtypeStruct((half, n_mb, 2) + rows, bf16),
                 jax.ShapeDtypeStruct((half, n_mb, 2) + shards, bf16),
+                jax.ShapeDtypeStruct((half, n_mb, expert_devs - 1) + shards[1:], bf16),
                 jax.ShapeDtypeStruct((3, half, d_loc, ff), bf16),
                 jax.ShapeDtypeStruct((3, half, d_loc, ff), bf16),
                 jax.ShapeDtypeStruct((3, half, ff, d_loc), bf16),
             ],
             in_specs=[hbm, vmem, vmem, hbm, hbm, hbm],
-            out_specs=[hbm] * 7,
+            out_specs=[hbm] * 8,
             scratch_shapes=[
                 pltpu.VMEM((4 * d_loc, ff), bf16),
                 pltpu.VMEM((4 * d_loc, ff), bf16),
@@ -520,7 +567,7 @@
                 dma((n_quad,)), dma((n_quad,)),
                 dma((2,)), dma((2,)), dma((2,)),
                 dma((2 * n_mb,)), dma((2 * n_mb,)),
-                dma((half, 2 * n_mb)), dma((half, n_mb)),
+                dma((half, 2 * n_mb)), dma((half, n_mb)), dma((half, n_mb, 2)), dma((half, n_mb)),
                 dma((2,)), dma((2,)),
             ],
             compiler_params=pltpu.CompilerParams(collective_id=0, has_side_effects=True, vmem_limit_bytes=62 * 1024 * 1024),

time: 927 us -> 953 us (1.028)
  Pallas kernels: 920 us -> 943 us
    pallas_call x1, Pallas kernels: 920 us -> 943 us  [per_device(): pl.pallas_call(functools.partial(moe_kernel, n_x, cap), out_shape=[jax.Sh...]
where the time goes in v4:
time: 953 us; the launch traced here: 948 us
  Pallas kernels  943 us (99%)
    pallas_call x1, Pallas kernels, per_device(): pl.pallas_call(functools.partial(moe_kernel, n_x, cap), out_shape=[jax.Sh...  943 us

profile of v4, /device:TPU:104, one launch (start us, length us, event | category | flops | bytes accessed | tf_op | source)
XLA Modules:
  0.0 947.5 jit_solution(8231135678258302178)
XLA Ops:
  0.0 942.7 %shard_map.64 = (bf16[2,8,64,2048]{3,2,1,0:T(8,128)(2,1)}, bf16[2,16,8,64,2048]{4,3,2,1,0:T(8,128)(2,1)}, bf16[4,2,2,8,64,2048]{5,4,3,2,1,0:T(8,128)(2,1)}, bf16...) custom-call(bf16[2,8,64,2048]{3,2,1,0:T(8,128)(2,1)} %bitcast.4, ...), custom_call_target="tpu_custom_call" | custom-call | tf_op jit(solution)/shard_map/pallas_call | solution.py:537
  942.7 4.8 copy.8

commit v5 on v3

--- a/solution.py
+++ b/solution.py
@@ -146,18 +146,14 @@
         pltpu.make_async_copy(rows_v.at[mb], x_slot(0, mb, 0, 0), xsem.at[mb]).start()
         acc_v[mb] = rows_v[mb].reshape(tok, d_model).astype(jnp.float32)
 
-    x_wait(0, 0, 3, 0)
-    x_start((0, 0, 2, 0), (0, 0, 3, 1))
-    x_wait(0, 0, 1, 0)
-    x_start((0, 0, 1, 1))
-    x_wait(1, 0, 0, 0)
-    x_start((1, 0, 3, 0), (1, 0, 1, 0), (1, 0, 0, 1))
-    x_wait(0, 1, 3, 0)
-    x_start((0, 1, 3, 1))
-    x_wait(0, 1, 1, 0)
-    x_start((0, 1, 2, 0), (0, 1, 1, 1))
-    x_wait(1, 1, 0, 0)
-    x_start((1, 1, 3, 0), (1, 1, 1, 0), (1, 1, 0, 1))
+    for mb in range(n_mb):
+        for r in (3, 1):
+            x_wait(0, mb, r, 0)
+            if r == 3 - 2 * mb:
+                x_start((0, mb, 2, 0))
+            x_start((0, mb, r, 1))
+        x_wait(1, mb, 0, 0)
+        x_start((1, mb, 3, 0), (1, mb, 1, 0), (1, mb, 0, 1))
     x_wait(0, 0, 2, 0)
     x_start((0, 0, 2, 1))
     x_wait(1, 0, 1, 0)
@@ -251,14 +247,15 @@
         dst = wd_v.at[(j + 1) % 4] if a == 2 else (wg_v, wu_v)[a].at[at, :]
         return pltpu.make_async_copy(src, dst, wl.at[j, a])
 
-    first, last = pl.ds(0, 3), pl.ds(3, 1)
-
-    def send(k, ck, cols):
+    parts = pl.ds(0, 3), pl.ds(3, 1)
+
+    def send(k, ck, part):
         line, mb = chunk_of(ck)
+        cols = parts[part]
 
         @pl.when(line == 1)
         def _():
-            remote(o_v.at[ck, 0, cols], bk_ref.at[k, mb, 1, 0, cols], b0.at[ck], br0.at[k, mb], partner).start()
+            remote(o_v.at[ck, 0, cols], bk_ref.at[k, mb, 1, 0, cols], b0.at[ck], br0.at[k, mb, part], partner).start()
 
         @pl.when(line == 0)
         def _():
@@ -267,7 +264,7 @@
         for rc in range(1, n_blk):
             r, cc = rc // 2, rc % 2
             back = ((n_x - r) % n_x) * 2 + cc
-            remote(o_v.at[ck, rc, cols], bk_ref.at[k, mb, line, back, cols], bs.at[ck], br.at[k, ck],
+            remote(o_v.at[ck, rc, cols], bk_ref.at[k, mb, line, back, cols], bs.at[ck], br.at[k, ck, part],
                    dev(line, r, cc)).start()
 
     def sent_wait(ck):
@@ -324,7 +321,7 @@
                 sent_wait(ck)
 
             down(ck, 0, 3)
-            send(k, ck, first)
+            send(k, ck, 0)
             return carry
 
         for j in (3, 0, 1):
@@ -336,7 +333,7 @@
 
         def down_chunk(ck, carry):
             down(ck, 3, 4)
-            send(k, ck, last)
+            send(k, ck, 1)
             return carry
 
         lax.fori_loop(0, n_chunk, down_chunk, 0)
@@ -344,42 +341,48 @@
     n_grp = n_blk // 4
     k_rows = 4 * cap
 
+    n_unit = 2 * n_chunk * n_grp
+
     def mix_of(u):
         v = u // n_grp
-        return v % 2, v // 2
-
-    def o_load(k, u):
-        line, mb = mix_of(u)
-        return pltpu.make_async_copy(bk_ref.at[k, mb, line, pl.ds((u % n_grp) * 4, 4)], ob_v.at[u % 2], osem.at[u % 2])
+        return v // n_chunk, v // n_mb % 2, v % n_mb
+
+    def o_load(k, u, part):
+        _, line, mb = mix_of(u)
+        cols = parts[part]
+        return pltpu.make_async_copy(bk_ref.at[k, mb, line, pl.ds((u % n_grp) * 4, 4), cols],
+                                     ob_v.at[u % 2, pl.ds(0, 4), cols], osem.at[u % 2])
 
     def o_ready(k, u):
-        line, mb = mix_of(u)
+        now, line, mb = mix_of(u)
         ck = (1 - line) * n_mb + mb
-
-        @pl.when(u % n_grp == 0)
-        def _():
-            many = bk_ref.at[k, mb, line, pl.ds(1, n_blk - 1)]
-            pltpu.make_async_copy(many, many, br.at[k, ck]).wait()
-
-        @pl.when(jnp.logical_and(u % n_grp == 0, line == 1))
-        def _():
-            one = bk_ref.at[k, mb, line, 0]
-            pltpu.make_async_copy(one, one, br0.at[k, mb]).wait()
-
-        o_load(k, u).start()
+        for part in range(2):
+            @pl.when(jnp.logical_and(u % n_grp == 0, now == part))
+            def _():
+                many = bk_ref.at[k, mb, line, pl.ds(1, n_blk - 1), parts[part]]
+                pltpu.make_async_copy(many, many, br.at[k, ck, part]).wait()
+
+                @pl.when(line == 1)
+                def _():
+                    one = bk_ref.at[k, mb, line, 0, parts[part]]
+                    pltpu.make_async_copy(one, one, br0.at[k, mb, part]).wait()
+
+            @pl.when(now == part)
+            def _():
+                o_load(k, u, part).start()
 
     def combine(k):
         o_ready(k, 0)
 
         def unit(u, carry):
-            line, mb = mix_of(u)
+            now, line, mb = mix_of(u)
             slot = u % 2
-            parts = []
+            mixes = []
             for i in range(4):
                 q = quad(line, (u % n_grp) * 4 + i)
                 hit = p_v[q, pl.ds(mb * half + k, 1), :] == place_i
-                parts.append(jnp.where(hit, g_v[q, pl.ds(mb * half + k, 1), :], 0.0))
-            mix = jnp.concatenate(parts, axis=0).T
+                mixes.append(jnp.where(hit, g_v[q, pl.ds(mb * half + k, 1), :], 0.0))
+            mix = jnp.concatenate(mixes, axis=0).T
             first = mix.astype(jnp.bfloat16)
             rest = mix - first.astype(jnp.float32)
             second = rest.astype(jnp.bfloat16)
@@ -387,7 +390,10 @@
             lt_v[:, 0:k_rows] = first
             lt_v[:, k_rows:2 * k_rows] = second
             lt_v[:, 2 * k_rows:3 * k_rows] = third
-            o_load(k, u).wait()
+            for part in range(2):
+                @pl.when(now == part)
+                def _():
+                    o_load(k, u, part).wait()
 
             @pl.when((u + 1) % n_grp != 0)
             def _():
@@ -406,20 +412,20 @@
                                               preferred_element_type=jnp.float32)
                 return carry
 
-            lax.fori_loop(0, d_model // n_tile, tile, 0)
-
-            @pl.when(jnp.logical_and((u + 1) % n_grp == 0, u + 1 < n_chunk * n_grp))
+            lax.fori_loop(now * 3 * n_part, (3 + now) * n_part, tile, 0)
+
+            @pl.when(jnp.logical_and((u + 1) % n_grp == 0, u + 1 < n_unit))
             def _():
                 o_ready(k, u + 1)
 
-            @pl.when(jnp.logical_and(k == half - 1, (u + 1) % (2 * n_grp) == 0))
+            @pl.when(jnp.logical_and(k == half - 1, u + 1 >= n_unit - (n_mb - 1 - mb) * n_grp))
             def _():
                 rows_v[mb] = acc_v[mb].astype(jnp.bfloat16).reshape(n_blk, cap, d_model)
                 pltpu.make_async_copy(rows_v.at[mb], y_ref.at[mb], ysem.at[mb]).start()
 
             return carry
 
-        lax.fori_loop(0, n_chunk * n_grp, unit, 0)
+        lax.fori_loop(0, n_unit, unit, 0)
 
     def step(k, carry):
         @pl.when(k < half)
@@ -520,7 +526,7 @@
                 dma((n_quad,)), dma((n_quad,)),
                 dma((2,)), dma((2,)), dma((2,)),
                 dma((2 * n_mb,)), dma((2 * n_mb,)),
-                dma((half, 2 * n_mb)), dma((half, n_mb)),
+                dma((half, 2 * n_mb, 2)), dma((half, n_mb, 2)),
                 dma((2,)), dma((2,)),
             ],
             compiler_params=pltpu.CompilerParams(collective_id=0, has_side_effects=True, vmem_limit_bytes=62 * 1024 * 1024),

time: 927 us -> 936 us (level)
  no operation moved by 1% of the time
where the time goes in v5:
time: 936 us; the launch traced here: 933 us
  Pallas kernels  928 us (99%)
    pallas_call x1, Pallas kernels, per_device(): pl.pallas_call(functools.partial(moe_kernel, n_x, cap), out_shape=[jax.Sh...  928 us

profile of v5, /device:TPU:104, one launch (start us, length us, event | category | flops | bytes accessed | tf_op | source)
XLA Modules:
  0.0 933.2 jit_solution(3082775724693900536)
XLA Ops:
  0.0 928.4 %shard_map.64 = (bf16[2,8,64,2048]{3,2,1,0:T(8,128)(2,1)}, bf16[2,16,8,64,2048]{4,3,2,1,0:T(8,128)(2,1)}, bf16[4,2,2,8,64,2048]{5,4,3,2,1,0:T(8,128)(2,1)}, bf16...) custom-call(bf16[2,8,64,2048]{3,2,1,0:T(8,128)(2,1)} %bitcast.4, ...), custom_call_target="tpu_custom_call" | custom-call | tf_op jit(solution)/shard_map/pallas_call | solution.py:497
  928.4 4.8 copy.8
